TPU v7x, 16 devices: a 4x2x1 block of a 4x4x8 slice. The times are simulated.
16 devices in a mesh: dp: 2 (over y, z), ep: 8 (over x, core).
Axes of the slice: x: 4, y: 2, z: 1, core: 2. Of those that a mesh axis runs over, the one named last changes fastest.
The devices are a block of a 4x4x8 slice.
Arguments:
- x: bfloat16 [2, 8, 256, 5120], P('dp', 'ep'), parts along dimension 0
- expert: int32 [2, 8, 256, 8], P('dp', 'ep'), parts along dimension 0
- slot: int32 [2, 8, 256, 8], P('dp', 'ep'), parts along dimension 0
- gate: float32 [2, 8, 256, 8], P('dp', 'ep'), parts along dimension 0
- w_gate: bfloat16 [40, 5120, 1536], P('ep')
- w_up: bfloat16 [40, 5120, 1536], P('ep')
- w_down: bfloat16 [40, 1536, 5120], P('ep')
- s_gate: bfloat16 [5120, 1536], replicated
- s_up: bfloat16 [5120, 1536], replicated
- s_down: bfloat16 [1536, 5120], replicated
Outputs:
- y: bfloat16 [2, 8, 256, 5120], P('dp', 'ep'), parts along dimension 0
There are 2 independent parts. A program takes and returns all parts, laid end to end along the dimension named above; an argument that names none is the same for every part.
All inputs are finite; a program needn't handle non-finite values.
Results may differ from a plain program's by a relative error of at most 0.009.
Values are sent between devices in bfloat16 or wider.
A program may use at most 768 MiB of HBM per device.

v0:
```python
import jax
import jax.numpy as jnp
from jax import lax
from jax.sharding import NamedSharding, PartitionSpec as P


def einsum(form, a, b):
    return jnp.einsum(form, a.astype(jnp.float32), b.astype(jnp.float32))


def for_all(x, s_gate, s_up, s_down):
    h = jax.nn.silu(einsum("...d,df->...f", x, s_gate)) * einsum("...d,df->...f", x, s_up)
    return einsum("...f,fd->...d", h.astype(jnp.bfloat16), s_down)


def solution(mesh):
    def placed(v, *spec):
        return lax.with_sharding_constraint(v, NamedSharding(mesh, P(*spec)))

    def step(x, expert, slot, gate, w_gate, w_up, w_down, s_gate, s_up, s_down):
        experts, (tokens, top) = w_gate.shape[0], expert.shape[2:]
        slots = 5 * tokens * top // (4 * experts)
        to_expert = jax.nn.one_hot(expert, experts, dtype=jnp.bfloat16)
        to_slot = jax.nn.one_hot(slot, slots, dtype=jnp.bfloat16)
        weighted = to_expert * gate[..., None].astype(jnp.bfloat16)
        dispatch = einsum("abtke,abtkc->abtec", to_expert, to_slot).astype(jnp.bfloat16)
        combine = einsum("abtke,abtkc->abtec", weighted, to_slot).astype(jnp.bfloat16)
        z = einsum("abtec,abtd->aebcd", dispatch, x).astype(jnp.bfloat16)
        z = placed(z, "dp", None, "ep", None, None)
        z = placed(z, "dp", "ep", None, None, None)
        h = jax.nn.silu(einsum("aebcd,edf->aebcf", z, w_gate))
        h = (h * einsum("aebcd,edf->aebcf", z, w_up)).astype(jnp.bfloat16)
        out = einsum("aebcf,efd->aebcd", h, w_down).astype(jnp.bfloat16)
        out = placed(out, "dp", "ep", None, None, None)
        out = placed(out, "dp", None, "ep", None, None)
        y = einsum("abtec,aebcd->abtd", combine, out)
        return (y + for_all(x, s_gate, s_up, s_down)).astype(jnp.bfloat16)

    return step
```

profile of v0, /device:TPU:112, one launch (start us, length us, event | category | flops | bytes accessed | tf_op | source)
XLA Modules:
  0.0 818.7 jit_solution(14413001771236778837)
XLA Ops:
  0.0 0.0 copy-start
  0.0 1.0 copy.11
  1.0 0.0 copy-start.1
  1.0 0.8 copy.9
  1.8 0.0 copy-start.3
  1.8 3.6 convolution_convert_fusion.1
  5.5 0.0 copy-done
  5.5 14.1 %convolution_convert_fusion = bf16[40,64,5120]{2,1,0:T(8,128)(2,1)} fusion(bf16[1,1,256,5120]{3,2,1,0:T(8,128)(2,1)S(1)} %copy-done, bf16[256,40,64]{2,1,0:T(8,128)(2,1)} %convolution_convert_fusion.1), kind=kOutput, calls=%fused_computation.18 | convolution fusion | flops 6723993600 | bytes 30146560 | tf_op jit(solution)/abtec,abtd->aebcd/dot_general | solution.py:8
  19.6 0.0 copy-done.1
  19.6 0.0 copy-done.3
  19.6 295.4 %all-to-all.4 = bf16[1,8,5,1,64,5120]{5,4,2,3,0,1:T(8,128)(2,1)} all-to-all(bf16[1,8,5,1,64,5120]{5,4,2,3,0,1:T(8,128)(2,1)} %bitcast.121), channel_id=1, replica_groups=mesh['dp'=2,'ep'=8] {'ep'}, dimensions={1} | all-to-all | bytes 52428800 | tf_op jit(solution)/sharding_constraint;jit(solution)/sharding_constraint | solution.py:18
  315.0 50.1 %fusion.2 = f32[5,8,64,1536]{3,2,1,0:T(8,128)} fusion(bf16[5,5120,1536]{2,1,0:T(8,128)(2,1)} %param.5, bf16[1,8,5,1,64,5120]{5,4,2,3,0,1:T(8,128)(2,1)} %all-to-all.4), kind=kOutput, calls=%fused_computation.2 | convolution fusion | flops 40265318400 | bytes 120586240 | tf_op jit(solution)/aebcd,edf->aebcf/dot_general | solution.py:8
  365.0 50.0 %fusion.4 = f32[5,8,64,1536]{3,2,1,0:T(8,128)} fusion(bf16[5,5120,1536]{2,1,0:T(8,128)(2,1)} %param.4, bf16[1,8,5,1,64,5120]{5,4,2,3,0,1:T(8,128)(2,1)} %all-to-all.4), kind=kOutput, calls=%fused_computation.4 | convolution fusion | flops 40265318400 | bytes 120586240 | tf_op jit(solution)/aebcd,edf->aebcf/dot_general | solution.py:8
  415.1 60.2 %convert_bitcast_fusion = bf16[1,5,8,1,64,5120]{5,4,2,1,3,0:T(8,128)(2,1)} fusion(bf16[5,1536,5120]{2,1,0:T(8,128)(2,1)} %param.6, f32[5,8,64,1536]{3,2,1,0:T(8,128)} %fusion.2, f32[5,8,64,1536]{3,2,1,0:T(8,128)} %fusion.4), kind=kOutput, calls=%fused_computation.8 | convolution fusion | flops 40302018560 | bytes 136314880 | tf_op jit(solution)/aebcf,efd->aebcd/dot_general | solution.py:8
  475.3 18.6 %copy.15 = bf16[1,5,8,1,64,5120]{5,4,1,3,0,2:T(8,128)(2,1)} copy(bf16[1,5,8,1,64,5120]{5,4,2,1,3,0:T(8,128)(2,1)} %convert_bitcast_fusion) | data formatting | bytes 52428800 | tf_op jit(solution)/sharding_constraint;jit(solution)/sharding_constraint | solution.py:18
  493.9 0.0 copy-start.5
  493.9 0.0 copy-start.2
  493.9 0.0 copy-start.4
  493.9 6.8 all-to-all-start.1
  500.8 0.0 copy-done.5
  500.8 0.1 copy.10
  500.9 0.0 copy-done.2
  500.9 0.0 copy-done.4
  500.9 4.2 convolution_convert_fusion.2
  505.1 8.8 %convolution_bitcast_fusion.2 = f32[1,1,256,1536]{3,2,1,0:T(8,128)} fusion(bf16[5120,1536]{1,0:T(8,128)(2,1)} %param.7, bf16[1,1,256,5120]{3,2,1,0:T(8,128)(2,1)S(1)} %copy-done), kind=kOutput, calls=%fused_computation.26 | convolution fusion | flops 4026531840 | bytes 19922944 | tf_op jit(solution)/...d,df->...f/dot_general | solution.py:8
  513.9 272.2 %all-to-all-done.1 = bf16[1,5,8,1,64,5120]{5,4,1,3,0,2:T(8,128)(2,1)} async-done(((bf16[1,5,8,1,64,5120]{5,4,1,3,0,2:T(8,128)(2,1)}), bf16[1,5,8,1,64,5120]{5,4,1,3,0,2:T(8,128)(2,1)}, u32[]{:S(2)}, u32[]{:S(2)}) %all-to-all-start.1) | async-done | bytes 26214432 | tf_op jit(solution)/sharding_constraint;jit(solution)/sharding_constraint | solution.py:18
  786.2 14.3 %convolution_bitcast_fusion = f32[256,5120]{1,0:T(8,128)} fusion(bf16[40,64,5120]{2,1,0:T(8,128)(2,1)} %bitcast.25, bf16[256,40,64]{2,1,0:T(8,128)(2,1)} %convolution_convert_fusion.2), kind=kOutput, calls=%fused_computation.20 | convolution fusion | flops 6710886400 | bytes 32768000 | tf_op jit(solution)/abtec,aebcd->abtd/dot_general | solution.py:8
  800.5 18.2 %fusion.19 = bf16[1,1,256,5120]{3,2,1,0:T(8,128)(2,1)} fusion(f32[256,5120]{1,0:T(8,128)} %convolution_bitcast_fusion, bf16[1536,5120]{1,0:T(8,128)(2,1)} %param.9, bf16[5120,1536]{1,0:T(8,128)(2,1)} %param.8, bf16[1,1,256,5120]{3,2,1,0:T(8,128)(2,1)S(1)} %copy-done, f32[1,1,256,1536]{3,2,1,0:T(8,128)} %convolution_bitcast_fusion.2), kind=kOutput, calls=%fused_computation.23 | convolution fusion | flops 8058044416 | bytes 43515904 | tf_op jit(solution)/...f,fd->...d/dot_general | solution.py:8
  (1 shorter events, 0.0 us)
Async XLA Ops:
  0.0 5.5 copy-start
  1.0 18.6 %copy-start.1 = (s32[256,8]{1,0:T(8,128)}, s32[256,8]{1,0:T(8,128)S(1)}, u32[]{:S(2)}) copy-start(s32[256,8]{1,0:T(8,128)S(1)} %copy.11) | copy-start | bytes 24580
  1.8 17.7 %copy-start.3 = (s32[256,8]{1,0:T(8,128)}, s32[256,8]{1,0:T(8,128)S(1)}, u32[]{:S(2)}) copy-start(s32[256,8]{1,0:T(8,128)S(1)} %copy.9) | copy-start | bytes 24580
  493.9 6.9 copy-start.5
  493.9 7.0 copy-start.2
  493.9 7.0 copy-start.4
  493.9 292.2 %all-to-all-start.1 = ((bf16[1,5,8,1,64,5120]{5,4,1,3,0,2:T(8,128)(2,1)}), bf16[1,5,8,1,64,5120]{5,4,1,3,0,2:T(8,128)(2,1)}, u32[]{:S(2)}, u32[]{:S(2)}) async-start(bf16[1,5,8,1,64,5120]{5,4,1,3,0,2:T(8,128)(2,1)} %copy.15), calls=%async_computation.1 | async-start | bytes 52428800 | tf_op jit(solution)/sharding_constraint;jit(solution)/sharding_constraint | solution.py:18
where the time goes:
time: 819 us
  blocking collectives  295 us (36%)
  waiting for transfers between devices  272 us (33%)
  matrix products  224 us (27%)
  local copies, waits for them, and re-layouts  20.6 us (3%)
    another operation x1, blocking collectives, placed(): return lax.with_sharding_constraint(v, NamedSharding(mesh, P(*spec)))  295 us
    another operation x1, waiting for transfers between devices, placed(): return lax.with_sharding_constraint(v, NamedSharding(mesh, P(*spec)))  272 us
    dot_general x9, matrix products, einsum(): return jnp.einsum(form, a.astype(jnp.float32), b.astype(jnp.float32))  224 us
    another operation x1, local copies, waits for them, and re-layouts, placed(): return lax.with_sharding_constraint(v, NamedSharding(mesh, P(*spec)))  18.6 us
  transfers between devices with their start and end apart: 1, of which 1 were waited for; matrix products, arithmetic and copies ran while one was open for 2% of the time, Pallas kernels for 0%

commit v1 on v0

v1 whole, which is shorter than its diff:
```python
import jax
import jax.numpy as jnp
from jax import lax
from jax.sharding import PartitionSpec as P

F32, BF16 = jnp.float32, jnp.bfloat16


def dot(form, a, b):
    return jnp.einsum(form, a, b, preferred_element_type=F32)


def solution(mesh):
    n = mesh.shape["ep"]

    def body(x, expert, slot, gate, w_gate, w_up, w_down, s_gate, s_up, s_down):
        x, expert, slot, gate = x[0, 0], expert[0, 0], slot[0, 0], gate[0, 0]
        (tokens, top), local = expert.shape, w_gate.shape[0]
        d, ff = w_gate.shape[1:]
        experts = local * n
        slots = 5 * tokens * top // (4 * experts)
        first = lax.axis_index("ep") * local
        meta = jnp.stack([expert.astype(F32), jnp.minimum(slot, slots).astype(F32), gate.astype(BF16).astype(F32)])
        meta = lax.all_gather(meta, "ep")
        xs = lax.all_gather(x, "ep")
        e = meta[:, 0].astype(jnp.int32) - first
        s = meta[:, 1].astype(jnp.int32)
        g = meta[:, 2].astype(BF16)
        ok = (e >= 0) & (e < local) & (s < slots)
        row = jnp.where(ok, e * slots + s, -1)
        hot = jax.nn.one_hot(row, local * slots, dtype=BF16)
        dispatch = jnp.sum(hot, axis=2).astype(BF16)
        combine = jnp.sum(hot * g[..., None], axis=2).astype(BF16)
        z = dot("btr,btd->brd", dispatch, xs).astype(BF16)
        z = z.reshape(n, local, slots, d)
        h = jax.nn.silu(dot("becd,edf->ebcf", z, w_gate))
        h = (h * dot("becd,edf->ebcf", z, w_up)).astype(BF16)
        hs = jax.nn.silu(dot("td,df->tf", x, s_gate))
        hs = (hs * dot("td,df->tf", x, s_up)).astype(BF16)
        shared = dot("tf,fd->td", hs, s_down)
        parts, w = [], d // 4
        for i in range(0, d, w):
            out = dot("ebcf,efd->becd", h, w_down[:, :, i : i + w]).astype(BF16)
            out = out.reshape(n, local * slots, w)
            y = dot("btr,brd->btd", combine, out).astype(BF16)
            parts.append(lax.psum_scatter(y, "ep", scatter_dimension=0, tiled=False))
        y = jnp.concatenate(parts, axis=-1).astype(F32)
        return (y + shared).astype(BF16)[None, None]

    a, e, r = P("dp", "ep", None, None), P("ep", None, None), P(None, None)
    return jax.shard_map(body, mesh=mesh, in_specs=(a, a, a, a, e, e, e, r, r, r), out_specs=a, check_vma=False)
```

time: 819 us -> 444 us (0.54)
  blocking collectives: 295 us -> 24.9 us
  waiting for transfers between devices: 272 us -> 118 us
  matrix products: 224 us -> 257 us
  between operations: 0.09 us -> 13.8 us
    another operation x1 -> x0, blocking collectives: 295 us -> none  [placed(): return lax.with_sharding_constraint(v, NamedSharding(mesh, P(*spec)))]
    another operation x1 -> x0, waiting for transfers between devices: 272 us -> none  [placed(): return lax.with_sharding_constraint(v, NamedSharding(mesh, P(*spec)))]
    all_gather x0 -> x1, waiting for transfers between devices: none -> 71.2 us  [body(): xs = lax.all_gather(x, 'ep')]
    reduce_scatter x0 -> x4, waiting for transfers between devices: none -> 46 us  [body(): parts.append(lax.psum_scatter(y, 'ep', scatter_dimension=0, tiled=False))]
    dot_general x9 -> x14, matrix products: 224 us -> 257 us  [dot(): return jnp.einsum(form, a, b, preferred_element_type=F32)]
    all_gather x0 -> x1, blocking collectives: none -> 24.9 us  [body(): meta = lax.all_gather(meta, 'ep')]
    another operation x1 -> x0, local copies, waits for them, and re-layouts: 18.6 us -> none  [placed(): return lax.with_sharding_constraint(v, NamedSharding(mesh, P(*spec)))]
    convert_element_type x1 -> x5, local copies, waits for them, and re-layouts: 0.12 us -> 14.4 us  [the longest x4 14.4 us: body(): out = dot('ebcf,efd->becd', h, w_down[:, :, i:i + w]).astype(BF16)]
  transfers between devices with their start and end apart: 1 -> 5, of which waited for: 1 -> 3; matrix products, arithmetic and copies ran while one was open for 2% -> 25% of each run, Pallas kernels for 0% -> 0%
where the time goes in v1:
time: 444 us; the launch traced here: 439 us
  matrix products  257 us (58%)
  waiting for transfers between devices  118 us (27%)
  blocking collectives  24.9 us (6%)
  local copies, waits for them, and re-layouts  16.9 us (4%)
  between operations  13.8 us (3%)
  other arithmetic  7.91 us (2%)
    dot_general x14, matrix products, dot(): return jnp.einsum(form, a, b, preferred_element_type=F32)  257 us
    all_gather x1, waiting for transfers between devices, body(): xs = lax.all_gather(x, 'ep')  71.2 us
    reduce_scatter x4, waiting for transfers between devices, body(): parts.append(lax.psum_scatter(y, 'ep', scatter_dimension=0, tiled=False))  46 us
    all_gather x1, blocking collectives, body(): meta = lax.all_gather(meta, 'ep')  24.9 us
    convert_element_type x4, local copies, waits for them, and re-layouts, body(): out = dot('ebcf,efd->becd', h, w_down[:, :, i:i + w]).astype(BF16)  14.4 us
  transfers between devices with their start and end apart: 5, of which 3 were waited for; matrix products, arithmetic and copies ran while one was open for 25% of the time, Pallas kernels for 0%

profile of v1, /device:TPU:112, one launch (start us, length us, event | category | flops | bytes accessed | tf_op | source)
XLA Modules:
  0.0 439.2 jit_solution(14419626996547123714)
XLA Ops:
  6.5 0.0 all-gather.4.cloned.1.call-start
  6.6 0.7 all-gather.4.cloned.1.call-update
  7.3 0.1 reduce-scatter.5.cloned.1.call-start
  7.4 0.7 bitcast_convert_fusion
  8.1 0.7 convert_bitcast_fusion.4
  8.8 24.9 %all-gather = f32[24,256,8]{1,2,0:T(8,128)S(1)} all-gather(f32[3,256,8]{1,2,0:T(8,128)S(1)} %pad_maximum_fusion), channel_id=2, replica_groups=mesh['dp'=2,'ep'=8] {'ep'}, dimensions={0}, use_global_device_ids=true | all-gather | bytes 221184 | tf_op jit(solution)/shard_map/all_gather | solution.py:24
  33.7 6.4 %fusion.26 = (bf16[8,256,320]{1,2,0:T(8,128)(2,1)S(1)}, bf16[8,256,320]{1,2,0:T(8,128)(2,1)}) fusion(s32[8,256,8]{1,2,0:T(8,128)S(1)} %select_bitcast_fusion, bf16[8,256,8]{1,2,0:T(8,128)(2,1)S(1)} %fusion.48), kind=kLoop, calls=%fused_computation.26 | loop fusion | flops 24903680 | bytes 2719744 | tf_op jit(solution)/shard_map/reduce_sum | solution.py:32
  40.2 71.2 %all-gather.4.cloned.1.call-done = bf16[8,1,256,5120]{3,2,1,0:T(8,128)(2,1)} async-done(((bf16[1,1,256,5120]{3,2,1,0:T(8,128)(2,1)}), bf16[8,1,256,5120]{3,2,1,0:T(8,128)(2,1)}) %all-gather.4.cloned.1.call-update) | async-done | bytes 20971536 | tf_op jit(solution)/shard_map/all_gather | solution.py:25
  111.4 25.4 %fusion.22 = bf16[8,320,5120]{2,1,0:T(8,128)(2,1)} fusion(bf16[8,256,320]{1,2,0:T(8,128)(2,1)S(1)} %get-tuple-element.5, bf16[8,1,256,5120]{3,2,1,0:T(8,128)(2,1)} %all-gather.4.cloned.1.call-done), kind=kOutput, calls=%fused_computation.24 | convolution fusion | flops 6723993600 | bytes 48496640 | tf_op jit(solution)/shard_map/btr,btd->brd/dot_general | solution.py:10
  136.8 50.1 %fusion.2 = f32[5,8,64,1536]{3,2,1,0:T(8,128)} fusion(bf16[5,5120,1536]{2,1,0:T(8,128)(2,1)} %param.14, bf16[8,5,64,5120]{3,2,1,0:T(8,128)(2,1)} %bitcast.100), kind=kOutput, calls=%fused_computation.2 | convolution fusion | flops 40265318400 | bytes 120586240 | tf_op jit(solution)/shard_map/becd,edf->ebcf/dot_general | solution.py:10
  186.8 55.1 %multiply_convert_fusion = bf16[5,8,64,1536]{3,2,1,0:T(8,128)(2,1)} fusion(f32[5,8,64,1536]{3,2,1,0:T(8,128)} %fusion.2, bf16[5,5120,1536]{2,1,0:T(8,128)(2,1)} %param.15, bf16[8,5,64,5120]{3,2,1,0:T(8,128)(2,1)} %bitcast.101), kind=kOutput, calls=%fused_computation.23 | convolution fusion | flops 40288911360 | bytes 128450560 | tf_op jit(solution)/shard_map/becd,edf->ebcf/dot_general | solution.py:10
  242.0 20.3 %convert_bitcast_fusion.3 = bf16[8,5,64,1280]{3,2,0,1:T(8,128)(2,1)} fusion(bf16[5,8,64,1536]{3,2,1,0:T(8,128)(2,1)} %multiply_convert_fusion, bf16[5,1536,5120]{2,1,0:T(8,128)(2,1)} %param.16), kind=kOutput, calls=%fused_computation.30 | convolution fusion | flops 10069606400 | bytes 34078720 | tf_op jit(solution)/shard_map/ebcf,efd->becd/dot_general | solution.py:10
  262.3 0.0 copy-start
  262.3 3.7 copy.35
  266.0 0.0 copy-done
  266.0 4.7 %convolution_convert_fusion.3 = bf16[8,256,1280]{2,1,0:T(8,128)(2,1)} fusion(bf16[8,256,320]{1,2,0:T(8,128)(2,1)S(1)} %copy-done, bf16[8,320,1280]{2,1,0:T(8,128)(2,1)S(1)} %bitcast.102), kind=kOutput, calls=%fused_computation.37 | convolution fusion | flops 1680343040 | bytes 13107200 | tf_op jit(solution)/shard_map/btr,brd->btd/dot_general | solution.py:10
  270.7 0.1 reduce-scatter.5.cloned.1.call-update
  270.7 0.1 reduce-scatter.7.cloned.1.call-start
  270.8 20.3 %convert_bitcast_fusion.2 = bf16[8,5,64,1280]{3,2,0,1:T(8,128)(2,1)} fusion(bf16[5,8,64,1536]{3,2,1,0:T(8,128)(2,1)} %multiply_convert_fusion, bf16[5,1536,5120]{2,1,0:T(8,128)(2,1)} %param.16), kind=kOutput, calls=%fused_computation.29 | convolution fusion | flops 10069606400 | bytes 34078720 | tf_op jit(solution)/shard_map/ebcf,efd->becd/dot_general | solution.py:10
  291.1 3.6 copy.36
  294.6 4.7 %convolution_convert_fusion.2 = bf16[8,256,1280]{2,1,0:T(8,128)(2,1)} fusion(bf16[8,256,320]{1,2,0:T(8,128)(2,1)S(1)} %copy-done, bf16[8,320,1280]{2,1,0:T(8,128)(2,1)S(1)} %bitcast.104), kind=kOutput, calls=%fused_computation.36 | convolution fusion | flops 1680343040 | bytes 13107200 | tf_op jit(solution)/shard_map/btr,brd->btd/dot_general | solution.py:10
  299.3 0.1 reduce-scatter.7.cloned.1.call-update
  299.4 0.1 reduce-scatter.9.cloned.1.call-start
  299.4 20.5 %convert_bitcast_fusion.1 = bf16[8,5,64,1280]{3,2,0,1:T(8,128)(2,1)} fusion(bf16[5,8,64,1536]{3,2,1,0:T(8,128)(2,1)} %multiply_convert_fusion, bf16[5,1536,5120]{2,1,0:T(8,128)(2,1)} %param.16), kind=kOutput, calls=%fused_computation.28 | convolution fusion | flops 10069606400 | bytes 34078720 | tf_op jit(solution)/shard_map/ebcf,efd->becd/dot_general | solution.py:10
  319.9 3.6 copy.37
  323.5 4.8 %convolution_convert_fusion.1 = bf16[8,256,1280]{2,1,0:T(8,128)(2,1)} fusion(bf16[8,256,320]{1,2,0:T(8,128)(2,1)S(1)} %copy-done, bf16[8,320,1280]{2,1,0:T(8,128)(2,1)S(1)} %bitcast.105), kind=kOutput, calls=%fused_computation.35 | convolution fusion | flops 1680343040 | bytes 13107200 | tf_op jit(solution)/shard_map/btr,brd->btd/dot_general | solution.py:10
  328.3 0.1 reduce-scatter.9.cloned.1.call-update
  328.3 0.1 reduce-scatter.11.cloned.1.call-start
  328.4 20.5 %convert_bitcast_fusion = bf16[8,5,64,1280]{3,2,0,1:T(8,128)(2,1)} fusion(bf16[5,8,64,1536]{3,2,1,0:T(8,128)(2,1)} %multiply_convert_fusion, bf16[5,1536,5120]{2,1,0:T(8,128)(2,1)} %param.16), kind=kOutput, calls=%fused_computation.27 | convolution fusion | flops 10069606400 | bytes 34078720 | tf_op jit(solution)/shard_map/ebcf,efd->becd/dot_general | solution.py:10
  348.9 3.6 copy.38
  352.5 4.7 %convolution_convert_fusion = bf16[8,256,1280]{2,1,0:T(8,128)(2,1)} fusion(bf16[8,256,320]{1,2,0:T(8,128)(2,1)S(1)} %copy-done, bf16[8,320,1280]{2,1,0:T(8,128)(2,1)S(1)} %bitcast.103), kind=kOutput, calls=%fused_computation.34 | convolution fusion | flops 1680343040 | bytes 13107200 | tf_op jit(solution)/shard_map/btr,brd->btd/dot_general | solution.py:10
  357.2 0.0 slice-start
  357.2 0.1 reduce-scatter.11.cloned.1.call-update
  357.3 0.0 copy-start.1
  357.3 0.0 slice-start.1
  357.3 0.0 slice-start.2
  357.3 0.0 slice-start.3
  357.3 8.9 %fusion.38 = f32[256,1536]{1,0:T(8,128)S(1)} fusion(bf16[5120,1536]{1,0:T(8,128)(2,1)} %param.17, bf16[1,1,256,5120]{3,2,1,0:T(8,128)(2,1)} %param.10), kind=kOutput, calls=%fused_computation.40 | convolution fusion | flops 4026531840 | bytes 19922944 | tf_op jit(solution)/shard_map/td,df->tf/dot_general | solution.py:10
  366.2 0.0 slice-done
  366.2 0.0 copy-done.1
  366.3 0.1 slice-done.1
  366.4 1.2 slice-done.2
  367.5 1.2 slice-done.3
  368.7 5.3 %fusion.40 = bf16[256,1536]{1,0:T(8,128)(2,1)} fusion(bf16[5120,1536]{1,0:T(8,128)(2,1)S(1)} %bitcast.109, bf16[1,1,256,5120]{3,2,1,0:T(8,128)(2,1)S(1)} %copy-done.1, f32[256,1536]{1,0:T(8,128)S(1)} %fusion.38), kind=kOutput, calls=%fused_computation.42 | convolution fusion | flops 4028891136 | bytes 20709376 | tf_op jit(solution)/shard_map/td,df->tf/dot_general | solution.py:10
  374.0 0.0 reduce-scatter.5.cloned.1.call-done
  374.0 0.0 reduce-scatter.7.cloned.1.call-done
  374.0 8.6 %reduce-scatter.9.cloned.1.call-done = bf16[1,256,1280]{2,1,0:T(8,128)(2,1)} async-done(((bf16[8,256,1280]{2,1,0:T(8,128)(2,1)}), bf16[1,256,1280]{2,1,0:T(8,128)(2,1)}) %reduce-scatter.9.cloned.1.call-update) | async-done | bytes 655376 | tf_op jit(solution)/shard_map/reduce_scatter | solution.py:46
  382.6 37.5 %reduce-scatter.11.cloned.1.call-done = bf16[1,256,1280]{2,1,0:T(8,128)(2,1)} async-done(((bf16[8,256,1280]{2,1,0:T(8,128)(2,1)}), bf16[1,256,1280]{2,1,0:T(8,128)(2,1)}) %reduce-scatter.11.cloned.1.call-update) | async-done | bytes 655376 | tf_op jit(solution)/shard_map/reduce_scatter | solution.py:46
  420.0 12.1 %fusion.28 = bf16[1,1,256,5120]{3,2,1,0:T(8,128)(2,1)} fusion(bf16[256,1536]{1,0:T(8,128)(2,1)} %fusion.40, bf16[1536,5120]{1,0:T(8,128)(2,1)} %param.19, bf16[256,1280]{1,0:T(8,128)(2,1)} %bitcast.113, bf16[256,1280]{1,0:T(8,128)(2,1)} %bitcast.112, bf16[256,1280]{1,0:T(8,128)(2,1)} %bitcast.111, bf16[256,1280]{1,0:T(8,128)(2,1)} %bitcast.110), kind=kOutput, calls=%fused_computation.33 | convolution fusion | flops 4039639040 | bytes 21757952 | tf_op jit(solution)/shard_map/tf,fd->td/dot_general | solution.py:10
  (4 shorter events, 0.0 us)
Async XLA Ops:
  6.5 104.8 %all-gather.4.cloned.1.call-start = ((), (), s32[]{:S(2)}) async-start(), calls=%async_computation.8 | async-start | bytes 23592960 | tf_op jit(solution)/shard_map/all_gather | solution.py:25
  7.3 366.7 %reduce-scatter.5.cloned.1.call-start = ((), (), s32[]{:S(2)}) async-start(), calls=%async_computation.4 | async-start | bytes 5898240 | tf_op jit(solution)/shard_map/reduce_scatter | solution.py:46
  262.3 3.7 copy-start
  270.7 103.3 %reduce-scatter.7.cloned.1.call-start = ((), (), s32[]{:S(2)}) async-start(), calls=%async_computation.5 | async-start | bytes 5898240 | tf_op jit(solution)/shard_map/reduce_scatter | solution.py:46
  299.4 83.2 %reduce-scatter.9.cloned.1.call-start = ((), (), s32[]{:S(2)}) async-start(), calls=%async_computation.6 | async-start | bytes 5898240 | tf_op jit(solution)/shard_map/reduce_scatter | solution.py:46
  328.3 91.7 %reduce-scatter.11.cloned.1.call-start = ((), (), s32[]{:S(2)}) async-start(), calls=%async_computation.7 | async-start | bytes 5898240 | tf_op jit(solution)/shard_map/reduce_scatter | solution.py:46
  357.2 9.0 %slice-start = ((s8[15728640]{0:T(1024)(128)(4,1)}), s8[3145728]{0:T(1024)(128)(4,1)S(1)}, s32[]{:S(2)}) async-start(s8[15728640]{0:T(1024)(128)(4,1)} %bitcast.108), calls=%async_computation.9 | async-start | bytes 6291456
  357.3 9.0 %copy-start.1 = (bf16[1,1,256,5120]{3,2,1,0:T(8,128)(2,1)S(1)}, bf16[1,1,256,5120]{3,2,1,0:T(8,128)(2,1)}, u32[]{:S(2)}) copy-start(bf16[1,1,256,5120]{3,2,1,0:T(8,128)(2,1)} %param.10) | copy-start | bytes 7864324
  357.3 9.1 %slice-start.1 = ((s8[15728640]{0:T(1024)(128)(4,1)}), s8[4194304]{0:T(1024)(128)(4,1)S(1)}, s32[]{:S(2)}) async-start(s8[15728640]{0:T(1024)(128)(4,1)} %bitcast.108), calls=%async_computation.10 | async-start | bytes 8388608
  357.3 10.3 %slice-start.2 = ((s8[15728640]{0:T(1024)(128)(4,1)}), s8[4194304]{0:T(1024)(128)(4,1)S(1)}, s32[]{:S(2)}) async-start(s8[15728640]{0:T(1024)(128)(4,1)} %bitcast.108), calls=%async_computation.11 | async-start | bytes 8388608
  357.3 11.4 %slice-start.3 = ((s8[15728640]{0:T(1024)(128)(4,1)}), s8[4194304]{0:T(1024)(128)(4,1)S(1)}, s32[]{:S(2)}) async-start(s8[15728640]{0:T(1024)(128)(4,1)} %bitcast.108), calls=%async_computation.12 | async-start | bytes 8388608
Sparse Core Ops, SparseCore 0:
  8.9 102.4 all-gather.3
  270.8 36.5 reduce-scatter.4
  309.8 35.3 reduce-scatter.6
  347.3 35.2 reduce-scatter.8
  384.7 35.2 reduce-scatter.10

commit v2 on v1

v2 whole, which is shorter than its diff:
```python
import functools

import jax
import jax.numpy as jnp
from jax import lax
from jax.experimental import pallas as pl
from jax.experimental.pallas import tpu as pltpu
from jax.sharding import PartitionSpec as P

F32, BF16 = jnp.float32, jnp.bfloat16
MESH = pl.DeviceIdType.MESH
ANY = pl.BlockSpec(memory_space=pl.ANY)
VM = pl.BlockSpec(memory_space=pltpu.VMEM)
WIDTH = 512
RING = 3


def mm(a, b):
    return jnp.dot(a, b, preferred_element_type=F32)


def silu(v):
    return v * (1.0 / (1.0 + jnp.exp(-v)))


def places(n):
    me = lax.axis_index("ep")
    chips = n // 2
    chip, core = lax.div(me, 2), lax.rem(me, 2)
    right, left = lax.rem(chip + 1, chips), lax.rem(chip + chips - 1, chips)
    across = lax.rem(chip + 2, chips)
    return me, chips, chip, core, right, left, across


def send(src, dst, send_sem, recv_sem, device):
    pltpu.make_async_remote_copy(
        src_ref=src, dst_ref=dst, send_sem=send_sem, recv_sem=recv_sem, device_id={"ep": device}, device_id_type=MESH
    ).start()


def wait(ref, sem):
    pltpu.make_async_copy(ref, ref, sem).wait()


def up_kernel(n, local, slots, x, mt, wg, wu, sg, su, h, hs, gt, xg, acc_g, acc_u, wbuf, xv, z, dm, gm, meta, hst,
              meta_send, meta_recv, own_send, fwd_send, pass_send, recv_l, recv_r, recv_a, recv_b, recv_p,
              wsem, xsem, ldsem, osem):
    me, chips, chip, core, right, left, across = places(n)
    dev_r, dev_l, dev_p = right * 2 + core, left * 2 + core, chip * 2 + 1 - core
    tokens, d = x.shape
    ff = sg.shape[1]
    chunks = d // WIDTH
    half = tokens // 2
    rows = n * slots
    top = mt.shape[0] // 4

    def cols(c):
        return pl.ds(pl.multiple_of(c * WIDTH, WIDTH), WIDTH)

    def fetch_shared(c):
        slot = lax.rem(c, RING)
        pltpu.make_async_copy(sg.at[cols(c), :], wbuf.at[slot, 0], wsem.at[slot]).start()
        pltpu.make_async_copy(su.at[cols(c), :], wbuf.at[slot, 1], wsem.at[slot]).start()

    def fetch(t):
        slot = lax.rem(t + chunks, RING)
        c, e = lax.div(t, local), lax.rem(t, local)
        pltpu.make_async_copy(wg.at[e, cols(c), :], wbuf.at[slot, 0], wsem.at[slot]).start()
        pltpu.make_async_copy(wu.at[e, cols(c), :], wbuf.at[slot, 1], wsem.at[slot]).start()

    fetch_shared(0)
    fetch_shared(1)

    def piece(c):
        return xv.at[c // 8, (c % 8) // 4, c % 4]

    for c in range(chunks):
        pltpu.make_async_copy(x.at[:, cols(c)], piece(c), xsem.at[c]).start()

    barrier = pltpu.get_barrier_semaphore()
    for r in range(1, n):
        pl.semaphore_signal(barrier, inc=1, device_id={"ep": lax.rem(me + r, n)}, device_id_type=MESH)
    pl.semaphore_wait(barrier, n - 1)

    mine = core * chips + chip

    def own(c):
        src, dst = x.at[:, cols(c)], xg.at[c, core, chip]
        send(src, dst, own_send.at[0], recv_l.at[c], dev_r)
        send(src, dst, own_send.at[1], recv_r.at[c], dev_l)
        send(src, dst, own_send.at[2], recv_p.at[c], dev_p)

    def forward(c):
        piece_l, piece_r = xg.at[c, core, left], xg.at[c, core, right]
        wait(piece_l, recv_l.at[c])
        upper = piece_l.at[pl.ds(0, half)]
        send(upper, upper, fwd_send.at[0], recv_a.at[c], dev_r)
        wait(piece_r, recv_r.at[c])
        lower = piece_r.at[pl.ds(half, half)]
        send(lower, lower, fwd_send.at[1], recv_b.at[c], dev_l)
        send(piece_l, piece_l, pass_send.at[0], recv_p.at[c], dev_p)
        send(piece_r, piece_r, pass_send.at[1], recv_p.at[c], dev_p)

    def last_hop(c):
        piece_o = xg.at[c, core, across]
        wait(piece_o.at[pl.ds(0, half)], recv_a.at[c])
        wait(piece_o.at[pl.ds(half, half)], recv_b.at[c])
        send(piece_o, piece_o, pass_send.at[2], recv_p.at[c], dev_p)

    def load(c):
        slot = lax.rem(c, 2)
        wait(xg.at[c, 1 - core], recv_p.at[c])
        pltpu.make_async_copy(xg.at[c, 1 - core], xv.at[slot, 1 - core], ldsem.at[slot]).start()
        pltpu.make_async_copy(x.at[:, cols(c)], xv.at[slot, core, chip], ldsem.at[slot]).start()
        for other in (left, right, across):
            pltpu.make_async_copy(xg.at[c, core, other], xv.at[slot, core, other], ldsem.at[slot]).start()

    own(0)
    for r in range(1, n):
        send(mt, meta.at[mine], meta_send.at[r], meta_recv.at[mine], lax.rem(me + r, n))
    meta[mine] = mt[...]

    tiles = [(i, min(i + WIDTH, ff)) for i in range(0, ff, WIDTH)]

    def shared_step(c):
        slot = c % RING
        wait(wbuf.at[slot], wsem.at[slot])
        if c + 2 < chunks:
            fetch_shared(c + 2)
        else:
            fetch(jnp.int32(c + 2 - chunks))
        wait(piece(c), xsem.at[c])
        xc = piece(c)[...]
        for lo, hi in tiles:
            for k, acc in ((0, acc_g), (1, acc_u)):
                v = mm(xc, wbuf[slot, k, :, lo:hi])
                acc[0, :tokens, lo:hi] = v if c == 0 else acc[0, :tokens, lo:hi] + v

    for c in range(chunks):
        if c == chunks - 2:
            forward(0)
            own(1)
        shared_step(c)
    hst[0, :tokens] = (silu(acc_g[0, :tokens]) * acc_u[0, :tokens]).astype(BF16)
    pltpu.make_async_copy(hst.at[0, pl.ds(0, tokens)], hs, osem.at[0]).start()

    for r in range(1, n):
        src = lax.rem(me + r, n)
        q = lax.rem(src, 2) * chips + lax.div(src, 2)
        wait(meta.at[q], meta_recv.at[q])
    first = (me * local).astype(F32)

    @pl.loop(0, n)
    def _(q):
        m = meta[q].astype(F32)
        e, s, g = m[0:top], m[top : 2 * top], m[2 * top : 3 * top]
        ok = (e >= first) & (e < first + local) & (s < slots)
        key = jnp.where(ok, (e - first) * slots + s, -1.0)
        for i in range(local):
            row = lax.broadcasted_iota(jnp.int32, (slots, tokens), 0).astype(F32) + float(i * slots)
            hot = jnp.zeros((slots, tokens), F32)
            weight = jnp.zeros((slots, tokens), F32)
            for k in range(top):
                hit = row == key[k : k + 1]
                hot = jnp.where(hit, 1.0, hot)
                weight = jnp.where(hit, g[k : k + 1], weight)
            dm[q, i * slots : (i + 1) * slots] = hot.astype(BF16)
            gm[q, i * slots : (i + 1) * slots] = weight.astype(BF16)

    last_hop(0)
    pltpu.make_async_copy(gm, gt, osem.at[1]).start()
    wait(hs, osem.at[0])
    load(0)

    def dispatch(c):
        slot = lax.rem(c, 2)
        wait(xv.at[slot], ldsem.at[slot])
        for q in range(n):
            v = mm(dm[q], xv[slot, q // chips, q % chips]).astype(BF16)
            for i in range(local):
                z[i, q * slots : (q + 1) * slots] = v[i * slots : (i + 1) * slots]

    steps = chunks * local

    @pl.loop(0, steps - local)
    def _(t):
        c, e = lax.div(t, local), lax.rem(t, local)
        slot = lax.rem(t + chunks, RING)

        @pl.when(e == 0)
        def _():
            dispatch(c)

        @pl.when(e == 1)
        def _():
            forward(c + 1)

            @pl.when(c + 2 < chunks)
            def _():
                own(c + 2)

        @pl.when(e == 3)
        def _():
            last_hop(c + 1)

        @pl.when(e == 4)
        def _():
            load(c + 1)

        wait(wbuf.at[slot], wsem.at[slot])
        fetch(t + 2)
        ze = z[e]
        for lo, hi in tiles:
            for k, acc in ((0, acc_g), (1, acc_u)):
                v = mm(ze, wbuf[slot, k, :, lo:hi])
                acc[e, :, lo:hi] = jnp.where(c == 0, 0.0, acc[e, :, lo:hi]) + v

    dispatch(jnp.int32(chunks - 1))

    @pl.loop(0, local)
    def _(e):
        t = steps - local + e
        slot = lax.rem(t + chunks, RING)
        wait(wbuf.at[slot], wsem.at[slot])

        @pl.when(e + 2 < local)
        def _():
            fetch(t + 2)

        to = lax.rem(e, 2)

        @pl.when(e >= 2)
        def _():
            wait(hst.at[to], osem.at[2 + to])

        ze = z[e]
        for lo, hi in tiles:
            g = acc_g[e, :, lo:hi] + mm(ze, wbuf[slot, 0, :, lo:hi])
            u = acc_u[e, :, lo:hi] + mm(ze, wbuf[slot, 1, :, lo:hi])
            hst[to, :, lo:hi] = (silu(g) * u).astype(BF16)
        pltpu.make_async_copy(hst.at[to], h.at[e], osem.at[2 + to]).start()

    for to in range(2):
        wait(hst.at[to], osem.at[2 + to])
    wait(gm, osem.at[1])
    for i in range(3):
        wait(x, own_send.at[i])
        wait(x, pass_send.at[i])
    for i in range(2):
        wait(x.at[pl.ds(0, half)], fwd_send.at[i])
    for r in range(1, n):
        wait(mt, meta_send.at[r])


def up(n, slots, x, mt, wg, wu, sg, su):
    tokens, d = x.shape
    local, _, ff = wg.shape
    chunks, rows, chips = d // WIDTH, n * slots, n // 2
    dma = pltpu.SemaphoreType.DMA
    flops = 2 * (rows * local + tokens) * d * ff * 2
    moved = 2 * (2 * local + 2) * d * ff
    return pl.pallas_call(
        functools.partial(up_kernel, n, local, slots),
        out_shape=[
            jax.ShapeDtypeStruct((local, rows, ff), BF16),
            jax.ShapeDtypeStruct((tokens, ff), BF16),
            jax.ShapeDtypeStruct((n, local * slots, tokens), BF16),
            jax.ShapeDtypeStruct((chunks, 2, chips, tokens, WIDTH), BF16),
        ],
        in_specs=[ANY, VM, ANY, ANY, ANY, ANY],
        out_specs=[ANY] * 4,
        scratch_shapes=[
            pltpu.VMEM((local, rows, ff), F32),
            pltpu.VMEM((local, rows, ff), F32),
            pltpu.VMEM((RING, 2, WIDTH, ff), BF16),
            pltpu.VMEM((2, 2, chips, tokens, WIDTH), BF16),
            pltpu.VMEM((local, rows, WIDTH), BF16),
            pltpu.VMEM((n, local * slots, tokens), BF16),
            pltpu.VMEM((n, local * slots, tokens), BF16),
            pltpu.VMEM((n, *mt.shape), BF16),
            pltpu.VMEM((2, rows, ff), BF16),
            dma((n,)), dma((n,)), dma((3,)), dma((2,)), dma((3,)),
            dma((chunks,)), dma((chunks,)), dma((chunks,)), dma((chunks,)), dma((chunks,)),
            dma((RING,)), dma((chunks,)), dma((2,)), dma((4,)),
        ],
        compiler_params=pltpu.CompilerParams(
            collective_id=0, has_side_effects=True, vmem_limit_bytes=62 * 2**20
        ),
        cost_estimate=pl.CostEstimate(flops=flops, bytes_accessed=moved, transcendentals=0),
    )(x, mt, wg, wu, sg, su)


def down_kernel(n, local, slots, h, hs, gt, wd, sd, y, hv, hsv, gm, wbuf, outs, part, sh, pair_s, pair_r, hop_s, hop_r,
                end_s, end_r, ys, insem, wsem, pair_ss, pair_rs, hop_ss, hop_rs, end_ss, end_rs, ysem):
    me, chips, chip, core, right, left, across = places(n)
    dev_r, dev_l, dev_p = right * 2 + core, left * 2 + core, chip * 2 + 1 - core
    tokens, ff = hs.shape
    chunks = wd.shape[2] // WIDTH
    half = tokens // 2
    per = local + 1
    steps = chunks * per

    def cols(c):
        return pl.ds(pl.multiple_of(c * WIDTH, WIDTH), WIDTH)

    def fetch(t):
        slot = lax.rem(t, RING)
        c, e = lax.div(t, per), lax.rem(t, per)

        @pl.when(e < local)
        def _():
            pltpu.make_async_copy(wd.at[e, :, cols(c)], wbuf.at[slot], wsem.at[slot]).start()

        @pl.when(e == local)
        def _():
            pltpu.make_async_copy(sd.at[:, cols(c)], wbuf.at[slot], wsem.at[slot]).start()

    fetch(jnp.int32(0))
    for e in range(local):
        pltpu.make_async_copy(h.at[e], hv.at[e], insem.at[e]).start()
    fetch(jnp.int32(1))
    pltpu.make_async_copy(hs, hsv, insem.at[local]).start()
    pltpu.make_async_copy(gt, gm, insem.at[local + 1]).start()

    barrier = pltpu.get_barrier_semaphore()
    for dev in (dev_r, dev_l, dev_p):
        pl.semaphore_signal(barrier, inc=1, device_id={"ep": dev}, device_id_type=MESH)
    pl.semaphore_wait(barrier, 3)

    def first_hop(c):
        k, b = lax.rem(c, 3), lax.rem(c, 2)

        @pl.when(c >= 2)
        def _():
            for i in range(2):
                wait(hop_s.at[b, i], hop_ss.at[b, i])

        wait(pair_r.at[c], pair_rs.at[c])
        v = (part[k, across] + pair_r[c, across].astype(F32)).astype(BF16)
        hop_s[b, 0] = v[:half]
        hop_s[b, 1] = v[half:]
        send(hop_s.at[b, 0], hop_r.at[c, 0], hop_ss.at[b, 0], hop_rs.at[c, 0], dev_r)
        send(hop_s.at[b, 1], hop_r.at[c, 1], hop_ss.at[b, 1], hop_rs.at[c, 1], dev_l)

    def second_hop(c):
        k, b = lax.rem(c, 3), lax.rem(c, 2)

        @pl.when(c >= 2)
        def _():
            for i in range(2):
                wait(end_s.at[b, i], end_ss.at[b, i])

        up, lo = pl.ds(0, half), pl.ds(half, half)
        for i, to in ((0, right), (1, left)):
            wait(hop_r.at[c, i], hop_rs.at[c, i])
            rows, others = (up, lo) if i == 0 else (lo, up)
            v = part[k, to, rows] + pair_r[c, to, rows].astype(F32) + hop_r[c, i].astype(F32)
            end_s[b, i, rows] = v.astype(BF16)
            v = part[k, to, others] + pair_r[c, to, others].astype(F32)
            end_s[b, i, others] = v.astype(BF16)
            send(end_s.at[b, i], end_r.at[c, i], end_ss.at[b, i], end_rs.at[c, i], (dev_r, dev_l)[i])

    def finish(c):
        k, b = lax.rem(c, 3), lax.rem(c, 2)

        @pl.when(c >= 2)
        def _():
            wait(ys.at[b], ysem.at[b])

        for i in range(2):
            wait(end_r.at[c, i], end_rs.at[c, i])
        v = part[k, chip] + pair_r[c, chip].astype(F32) + end_r[c, 0].astype(F32) + end_r[c, 1].astype(F32)
        ys[b] = (v + sh[k]).astype(BF16)
        pltpu.make_async_copy(ys.at[b], y.at[:, cols(c)], ysem.at[b]).start()

    @pl.loop(0, steps)
    def _(t):
        c, e = lax.div(t, per), lax.rem(t, per)
        slot = lax.rem(t, RING)

        @pl.when((e == 1) & (c >= 1))
        def _():
            first_hop(c - 1)

        @pl.when((e == 2) & (c >= 2))
        def _():
            second_hop(c - 2)

        @pl.when((e == 4) & (c >= 3))
        def _():
            finish(c - 3)

        @pl.when((c == 0) & (e < local))
        def _():
            wait(hv.at[e], insem.at[e])

        @pl.when(t == local)
        def _():
            wait(hs, insem.at[local])
            wait(gt, insem.at[local + 1])

        wait(wbuf.at[slot], wsem.at[slot])

        @pl.when(t + 2 < steps)
        def _():
            fetch(t + 2)

        @pl.when(e < local)
        def _():
            v = mm(hv[e], wbuf[slot]).astype(BF16)
            for q in range(n):
                outs[q, pl.ds(pl.multiple_of(e * slots, slots), slots)] = v[q * slots : (q + 1) * slots]

        @pl.when(e == local)
        def _():
            b, k = lax.rem(c, 2), lax.rem(c, 3)

            @pl.when(c >= 2)
            def _():
                wait(pair_s.at[b], pair_ss.at[b])

            def combined(q):
                return lax.dot_general(gm[q], outs[q], (((0,), (0,)), ((), ())), preferred_element_type=F32)

            for i in range(chips):
                pair_s[b, i] = combined((1 - core) * chips + i).astype(BF16)
            send(pair_s.at[b], pair_r.at[c], pair_ss.at[b], pair_rs.at[c], dev_p)
            for i in range(chips):
                part[k, i] = combined(core * chips + i)
            sh[k] = mm(hsv[...], wbuf[slot])

    end = chunks - 1
    second_hop(jnp.int32(end - 1))
    first_hop(jnp.int32(end))
    finish(jnp.int32(end - 2))
    second_hop(jnp.int32(end))
    finish(jnp.int32(end - 1))
    finish(jnp.int32(end))
    for b in range(2):
        wait(pair_s.at[b], pair_ss.at[b])
        wait(ys.at[b], ysem.at[b])
        for i in range(2):
            wait(hop_s.at[b, i], hop_ss.at[b, i])
            wait(end_s.at[b, i], end_ss.at[b, i])


def down(n, slots, h, hs, gt, wd, sd):
    local, rows, ff = h.shape
    tokens, d = hs.shape[0], wd.shape[2]
    chunks, chips, half = d // WIDTH, n // 2, tokens // 2
    dma = pltpu.SemaphoreType.DMA
    flops = 2 * (rows * local + tokens) * d * ff
    return pl.pallas_call(
        functools.partial(down_kernel, n, local, slots),
        out_shape=jax.ShapeDtypeStruct((tokens, d), BF16),
        in_specs=[ANY] * 5,
        out_specs=ANY,
        scratch_shapes=[
            pltpu.VMEM(h.shape, BF16),
            pltpu.VMEM(hs.shape, BF16),
            pltpu.VMEM(gt.shape, BF16),
            pltpu.VMEM((RING, ff, WIDTH), BF16),
            pltpu.VMEM((n, local * slots, WIDTH), BF16),
            pltpu.VMEM((3, chips, tokens, WIDTH), F32),
            pltpu.VMEM((3, tokens, WIDTH), F32),
            pltpu.VMEM((2, chips, tokens, WIDTH), BF16),
            pltpu.VMEM((chunks, chips, tokens, WIDTH), BF16),
            pltpu.VMEM((2, 2, half, WIDTH), BF16),
            pltpu.VMEM((chunks, 2, half, WIDTH), BF16),
            pltpu.VMEM((2, 2, tokens, WIDTH), BF16),
            pltpu.VMEM((chunks, 2, tokens, WIDTH), BF16),
            pltpu.VMEM((2, tokens, WIDTH), BF16),
            dma((local + 2,)), dma((RING,)), dma((2,)), dma((chunks,)), dma((2, 2)), dma((chunks, 2)),
            dma((2, 2)), dma((chunks, 2)), dma((2,)),
        ],
        compiler_params=pltpu.CompilerParams(
            collective_id=1, has_side_effects=True, vmem_limit_bytes=62 * 2**20
        ),
        cost_estimate=pl.CostEstimate(flops=flops, bytes_accessed=2 * (local + 1) * d * ff, transcendentals=0),
    )(h, hs, gt, wd, sd)


def solution(mesh):
    n = mesh.shape["ep"]

    def body(x, expert, slot, gate, w_gate, w_up, w_down, s_gate, s_up, s_down):
        x, expert, slot, gate = x[0, 0], expert[0, 0], slot[0, 0], gate[0, 0]
        (tokens, top), local = expert.shape, w_gate.shape[0]
        slots = 5 * tokens * top // (4 * local * n)
        parts = [expert.astype(BF16), jnp.minimum(slot, slots).astype(BF16), gate.astype(BF16)]
        mt = jnp.concatenate([p.T for p in parts] + [jnp.zeros((top, tokens), BF16)])
        h, hs, gt, _ = up(n, slots, x, mt, w_gate, w_up, s_gate, s_up)
        return down(n, slots, h, hs, gt, w_down, s_down)[None, None]

    a, e, r = P("dp", "ep", None, None), P("ep", None, None), P(None, None)
    return jax.shard_map(body, mesh=mesh, in_specs=(a, a, a, a, e, e, e, r, r, r), out_specs=a, check_vma=False)
```

time: 444 us -> 258 us (0.58); the launches traced: 439 us -> 258 us
  matrix products: 257 us -> 0 us
  Pallas kernels: 0 us -> 252 us
  waiting for transfers between devices: 118 us -> 0 us
  blocking collectives: 24.9 us -> 0 us
  between operations: 13.8 us -> 0.02 us
  local copies, waits for them, and re-layouts: 16.9 us -> 3.48 us
  other arithmetic: 7.91 us -> 2.1 us
    dot_general x14 -> x0, matrix products: 257 us -> none  [dot(): return jnp.einsum(form, a, b, preferred_element_type=F32)]
    pallas_call x0 -> x2, Pallas kernels: none -> 252 us  [the longest x1 146 us: up(): pl.pallas_call(functools.partial(up_kernel, n, local, slots), out_shape=[...]
    all_gather x1 -> x0, waiting for transfers between devices: 71.2 us -> none  [body(): xs = lax.all_gather(x, 'ep')]
    reduce_scatter x4 -> x0, waiting for transfers between devices: 46 us -> none  [body(): parts.append(lax.psum_scatter(y, 'ep', scatter_dimension=0, tiled=False))]
    all_gather x1 -> x0, blocking collectives: 24.9 us -> none  [body(): meta = lax.all_gather(meta, 'ep')]
    convert_element_type x5 -> x0, local copies, waits for them, and re-layouts: 14.4 us -> none  [the longest x4 14.4 us: body(): out = dot('ebcf,efd->becd', h, w_down[:, :, i:i + w]).astype(BF16)]
    reduce_sum x1 -> x0, other arithmetic: 6.45 us -> none  [body(): dispatch = jnp.sum(hot, axis=2).astype(BF16)]
  transfers between devices with their start and end apart: 5 -> 0, of which waited for: 3 -> 0; matrix products, arithmetic and copies ran while one was open for 25% -> 0% of each run, Pallas kernels for 0% -> 0%
where the time goes in v2:
time: 258 us
  Pallas kernels  252 us (98%)
  local copies, waits for them, and re-layouts  3.48 us (1%)
    pallas_call x1, Pallas kernels, up(): pl.pallas_call(functools.partial(up_kernel, n, local, slots), out_shape=[...  146 us
    pallas_call x1, Pallas kernels, down(): pl.pallas_call(functools.partial(down_kernel, n, local, slots), out_shape...  106 us

profile of v2, /device:TPU:112, one launch (start us, length us, event | category | flops | bytes accessed | tf_op | source)
XLA Modules:
  0.0 257.8 jit_solution(11605594555723845994)
XLA Ops:
  0.0 0.1 pad.3.clone
  0.1 0.7 convert_bitcast_fusion
  0.8 0.7 fusion
  1.5 0.7 maximum_maximum_fusion.mt
  2.2 146.2 %shard_map.100 = (bf16[5,512,1536]{2,1,0:T(8,128)(2,1)}, bf16[256,1536]{1,0:T(8,128)(2,1)}, bf16[8,320,256]{2,1,0:T(8,128)(2,1)}, bf16[10,2,4,256,512]{4,3,2,1,0:T(8,128)(2,1)}) custom-call(bf16[256,5120]{1,0:T(8,128)(2,1)} %bitcast.15, bf16[32,256]{1,0:T(8,128)(2,1)} %maximum_maximum_fusion.mt, bf16[5,5120,1536]{2,1,0:T(8,128)(2,1)} %wg.1, ...), custom_call_target="tpu_custom_call" | custom-call | flops 88583700480 | bytes 188743680 | tf_op jit(solution)/shard_map/pallas_call | solution.py:262
  148.3 106.1 %shard_map.101 = bf16[256,5120]{1,0:T(8,128)(2,1)} custom-call(bf16[5,512,1536]{2,1,0:T(8,128)(2,1)} %get-tuple-element.8.h, bf16[256,1536]{1,0:T(8,128)(2,1)} %get-tuple-element.9.hs, bf16[8,320,256]{2,1,0:T(8,128)(2,1)} %get-tuple-element.10.gt, bf16[5,1536,5120]{2,1,0:T(8,128)(2,1)} %wd.1, bf16[1536,5120]{1,0:T(8,128)(2,1)} %sd.1), custom_call_target="tpu_custom_call" | custom-call | flops 44291850240 | bytes 94371840 | tf_op jit(solution)/shard_map/pallas_call | solution.py:453
  254.4 3.4 %copy.12 = bf16[1,1,256,5120]{3,2,1,0:T(8,128)(2,1)} copy(bf16[1,1,256,5120]{3,2,1,0:T(8,128)(2,1)} %bitcast.14) | data formatting | bytes 5242880
  (1 shorter events, 0.0 us)

commit v3 on v2

--- a/solution.py
+++ b/solution.py
@@ -12,6 +12,8 @@
 ANY = pl.BlockSpec(memory_space=pl.ANY)
 VM = pl.BlockSpec(memory_space=pltpu.VMEM)
 WIDTH = 512
+TILE = 256
+DOWN = 512
 RING = 3
 
 
@@ -58,18 +60,16 @@
         return pl.ds(pl.multiple_of(c * WIDTH, WIDTH), WIDTH)
 
     def fetch_shared(c):
-        slot = lax.rem(c, RING)
+        slot = c % local
         pltpu.make_async_copy(sg.at[cols(c), :], wbuf.at[slot, 0], wsem.at[slot]).start()
         pltpu.make_async_copy(su.at[cols(c), :], wbuf.at[slot, 1], wsem.at[slot]).start()
 
-    def fetch(t):
-        slot = lax.rem(t + chunks, RING)
-        c, e = lax.div(t, local), lax.rem(t, local)
-        pltpu.make_async_copy(wg.at[e, cols(c), :], wbuf.at[slot, 0], wsem.at[slot]).start()
-        pltpu.make_async_copy(wu.at[e, cols(c), :], wbuf.at[slot, 1], wsem.at[slot]).start()
-
-    fetch_shared(0)
-    fetch_shared(1)
+    def fetch_at(c, e):
+        pltpu.make_async_copy(wg.at[e, cols(c), :], wbuf.at[e, 0], wsem.at[e]).start()
+        pltpu.make_async_copy(wu.at[e, cols(c), :], wbuf.at[e, 1], wsem.at[e]).start()
+
+    for i in range(local):
+        fetch_shared(i)
 
     def piece(c):
         return xv.at[c // 8, (c % 8) // 4, c % 4]
@@ -84,8 +84,9 @@
 
     mine = core * chips + chip
 
-    def own(c):
-        src, dst = x.at[:, cols(c)], xg.at[c, core, chip]
+    def own(c, i):
+        part = pl.ds(i * half, half)
+        src, dst = x.at[part, cols(c)], xg.at[c, core, chip, part]
         send(src, dst, own_send.at[0], recv_l.at[c], dev_r)
         send(src, dst, own_send.at[1], recv_r.at[c], dev_l)
         send(src, dst, own_send.at[2], recv_p.at[c], dev_p)
@@ -115,20 +116,21 @@
         for other in (left, right, across):
             pltpu.make_async_copy(xg.at[c, core, other], xv.at[slot, core, other], ldsem.at[slot]).start()
 
-    own(0)
+    own(0, 0)
+    own(0, 1)
     for r in range(1, n):
         send(mt, meta.at[mine], meta_send.at[r], meta_recv.at[mine], lax.rem(me + r, n))
     meta[mine] = mt[...]
 
-    tiles = [(i, min(i + WIDTH, ff)) for i in range(0, ff, WIDTH)]
+    tiles = [(i, min(i + TILE, ff)) for i in range(0, ff, TILE)]
 
     def shared_step(c):
-        slot = c % RING
+        slot = c % local
         wait(wbuf.at[slot], wsem.at[slot])
-        if c + 2 < chunks:
-            fetch_shared(c + 2)
-        else:
-            fetch(jnp.int32(c + 2 - chunks))
+        if c >= 1 and c + local - 1 < chunks:
+            fetch_shared(c + local - 1)
+        elif c >= 1 and c + local - 1 - chunks < local - 2:
+            fetch_at(0, c + local - 1 - chunks)
         wait(piece(c), xsem.at[c])
         xc = piece(c)[...]
         for lo, hi in tiles:
@@ -139,7 +141,9 @@
     for c in range(chunks):
         if c == chunks - 2:
             forward(0)
-            own(1)
+            own(1, 0)
+            own(1, 1)
+            own(2, 0)
         shared_step(c)
     hst[0, :tokens] = (silu(acc_g[0, :tokens]) * acc_u[0, :tokens]).astype(BF16)
     pltpu.make_async_copy(hst.at[0, pl.ds(0, tokens)], hs, osem.at[0]).start()
@@ -180,63 +184,53 @@
             for i in range(local):
                 z[i, q * slots : (q + 1) * slots] = v[i * slots : (i + 1) * slots]
 
-    steps = chunks * local
-
-    @pl.loop(0, steps - local)
-    def _(t):
-        c, e = lax.div(t, local), lax.rem(t, local)
-        slot = lax.rem(t + chunks, RING)
-
-        @pl.when(e == 0)
-        def _():
-            dispatch(c)
-
-        @pl.when(e == 1)
-        def _():
-            forward(c + 1)
-
-            @pl.when(c + 2 < chunks)
-            def _():
-                own(c + 2)
-
-        @pl.when(e == 3)
-        def _():
-            last_hop(c + 1)
-
-        @pl.when(e == 4)
-        def _():
-            load(c + 1)
-
+    @pl.loop(0, chunks - 1)
+    def _(c):
+        forward(c + 1)
+
+        @pl.when(c + 2 < chunks)
+        def _():
+            own(c + 2, 1)
+
+        @pl.when(c + 3 < chunks)
+        def _():
+            own(c + 3, 0)
+
+        start, groups = 0, (local - 2, 1, 1)
+        for i, size in enumerate(groups):
+            group = range(start, start + size)
+            start += size
+            if i == 1:
+                last_hop(c + 1)
+            if i == 2:
+                load(c + 1)
+            for e in group:
+                wait(wbuf.at[e], wsem.at[e])
+            if i == 0:
+                for e in range(local - 2, local):
+                    fetch_at(c, e)
+                dispatch(c)
+            if i == 1:
+                for e in range(local - 2):
+                    fetch_at(c + 1, e)
+            for e in group:
+                for lo, hi in tiles:
+                    for k, acc in ((0, acc_g), (1, acc_u)):
+                        v = mm(z[e], wbuf[e, k, :, lo:hi])
+                        acc[e, :, lo:hi] = jnp.where(c == 0, 0.0, acc[e, :, lo:hi]) + v
+
+    for e in range(local - 2, local):
+        fetch_at(chunks - 1, e)
+    dispatch(jnp.int32(chunks - 1))
+
+    for e in range(local):
+        slot, to = e, e % 2
         wait(wbuf.at[slot], wsem.at[slot])
-        fetch(t + 2)
-        ze = z[e]
+        if e >= 2:
+            wait(hst.at[to], osem.at[2 + to])
         for lo, hi in tiles:
-            for k, acc in ((0, acc_g), (1, acc_u)):
-                v = mm(ze, wbuf[slot, k, :, lo:hi])
-                acc[e, :, lo:hi] = jnp.where(c == 0, 0.0, acc[e, :, lo:hi]) + v
-
-    dispatch(jnp.int32(chunks - 1))
-
-    @pl.loop(0, local)
-    def _(e):
-        t = steps - local + e
-        slot = lax.rem(t + chunks, RING)
-        wait(wbuf.at[slot], wsem.at[slot])
-
-        @pl.when(e + 2 < local)
-        def _():
-            fetch(t + 2)
-
-        to = lax.rem(e, 2)
-
-        @pl.when(e >= 2)
-        def _():
-            wait(hst.at[to], osem.at[2 + to])
-
-        ze = z[e]
-        for lo, hi in tiles:
-            g = acc_g[e, :, lo:hi] + mm(ze, wbuf[slot, 0, :, lo:hi])
-            u = acc_u[e, :, lo:hi] + mm(ze, wbuf[slot, 1, :, lo:hi])
+            g = acc_g[e, :, lo:hi] + mm(z[e], wbuf[slot, 0, :, lo:hi])
+            u = acc_u[e, :, lo:hi] + mm(z[e], wbuf[slot, 1, :, lo:hi])
             hst[to, :, lo:hi] = (silu(g) * u).astype(BF16)
         pltpu.make_async_copy(hst.at[to], h.at[e], osem.at[2 + to]).start()
 
@@ -272,7 +266,7 @@
         scratch_shapes=[
             pltpu.VMEM((local, rows, ff), F32),
             pltpu.VMEM((local, rows, ff), F32),
-            pltpu.VMEM((RING, 2, WIDTH, ff), BF16),
+            pltpu.VMEM((local, 2, WIDTH, ff), BF16),
             pltpu.VMEM((2, 2, chips, tokens, WIDTH), BF16),
             pltpu.VMEM((local, rows, WIDTH), BF16),
             pltpu.VMEM((n, local * slots, tokens), BF16),
@@ -281,10 +275,10 @@
             pltpu.VMEM((2, rows, ff), BF16),
             dma((n,)), dma((n,)), dma((3,)), dma((2,)), dma((3,)),
             dma((chunks,)), dma((chunks,)), dma((chunks,)), dma((chunks,)), dma((chunks,)),
-            dma((RING,)), dma((chunks,)), dma((2,)), dma((4,)),
+            dma((local,)), dma((chunks,)), dma((2,)), dma((4,)),
         ],
         compiler_params=pltpu.CompilerParams(
-            collective_id=0, has_side_effects=True, vmem_limit_bytes=62 * 2**20
+            collective_id=0, has_side_effects=True, vmem_limit_bytes=66 * 10**6
         ),
         cost_estimate=pl.CostEstimate(flops=flops, bytes_accessed=moved, transcendentals=0),
     )(x, mt, wg, wu, sg, su)
@@ -295,13 +289,13 @@
     me, chips, chip, core, right, left, across = places(n)
     dev_r, dev_l, dev_p = right * 2 + core, left * 2 + core, chip * 2 + 1 - core
     tokens, ff = hs.shape
-    chunks = wd.shape[2] // WIDTH
+    chunks = wd.shape[2] // DOWN
     half = tokens // 2
     per = local + 1
     steps = chunks * per
 
     def cols(c):
-        return pl.ds(pl.multiple_of(c * WIDTH, WIDTH), WIDTH)
+        return pl.ds(pl.multiple_of(c * DOWN, DOWN), DOWN)
 
     def fetch(t):
         slot = lax.rem(t, RING)
@@ -447,7 +441,7 @@
 def down(n, slots, h, hs, gt, wd, sd):
     local, rows, ff = h.shape
     tokens, d = hs.shape[0], wd.shape[2]
-    chunks, chips, half = d // WIDTH, n // 2, tokens // 2
+    chunks, chips, half = d // DOWN, n // 2, tokens // 2
     dma = pltpu.SemaphoreType.DMA
     flops = 2 * (rows * local + tokens) * d * ff
     return pl.pallas_call(
@@ -459,17 +453,17 @@
             pltpu.VMEM(h.shape, BF16),
             pltpu.VMEM(hs.shape, BF16),
             pltpu.VMEM(gt.shape, BF16),
-            pltpu.VMEM((RING, ff, WIDTH), BF16),
-            pltpu.VMEM((n, local * slots, WIDTH), BF16),
-            pltpu.VMEM((3, chips, tokens, WIDTH), F32),
-            pltpu.VMEM((3, tokens, WIDTH), F32),
-            pltpu.VMEM((2, chips, tokens, WIDTH), BF16),
-            pltpu.VMEM((chunks, chips, tokens, WIDTH), BF16),
-            pltpu.VMEM((2, 2, half, WIDTH), BF16),
-            pltpu.VMEM((chunks, 2, half, WIDTH), BF16),
-            pltpu.VMEM((2, 2, tokens, WIDTH), BF16),
-            pltpu.VMEM((chunks, 2, tokens, WIDTH), BF16),
-            pltpu.VMEM((2, tokens, WIDTH), BF16),
+            pltpu.VMEM((RING, ff, DOWN), BF16),
+            pltpu.VMEM((n, local * slots, DOWN), BF16),
+            pltpu.VMEM((3, chips, tokens, DOWN), F32),
+            pltpu.VMEM((3, tokens, DOWN), F32),
+            pltpu.VMEM((2, chips, tokens, DOWN), BF16),
+            pltpu.VMEM((chunks, chips, tokens, DOWN), BF16),
+            pltpu.VMEM((2, 2, half, DOWN), BF16),
+            pltpu.VMEM((chunks, 2, half, DOWN), BF16),
+            pltpu.VMEM((2, 2, tokens, DOWN), BF16),
+            pltpu.VMEM((chunks, 2, tokens, DOWN), BF16),
+            pltpu.VMEM((2, tokens, DOWN), BF16),
             dma((local + 2,)), dma((RING,)), dma((2,)), dma((chunks,)), dma((2, 2)), dma((chunks, 2)),
             dma((2, 2)), dma((chunks, 2)), dma((2,)),
         ],

time: 258 us -> 242 us (0.938)
  Pallas kernels: 252 us -> 236 us
    pallas_call x1, Pallas kernels: 146 us -> 129 us  [up(): pl.pallas_call(functools.partial(up_kernel, n, local, slots), out_shape=[...]
where the time goes in v3:
time: 242 us; the launch traced here: 241 us
  Pallas kernels  236 us (98%)
  local copies, waits for them, and re-layouts  3.48 us (1%)
    pallas_call x1, Pallas kernels, up(): pl.pallas_call(functools.partial(up_kernel, n, local, slots), out_shape=[...  129 us
    pallas_call x1, Pallas kernels, down(): pl.pallas_call(functools.partial(down_kernel, n, local, slots), out_shape...  106 us

profile of v3, /device:TPU:112, one launch (start us, length us, event | category | flops | bytes accessed | tf_op | source)
XLA Modules:
  0.0 241.3 jit_solution(17642202197388083985)
XLA Ops:
  0.0 0.1 pad.3.clone
  0.1 0.7 convert_bitcast_fusion
  0.8 0.7 fusion
  1.5 0.7 maximum_maximum_fusion.mt
  2.2 129.3 %shard_map.100 = (bf16[5,512,1536]{2,1,0:T(8,128)(2,1)}, bf16[256,1536]{1,0:T(8,128)(2,1)}, bf16[8,320,256]{2,1,0:T(8,128)(2,1)}, bf16[10,2,4,256,512]{4,3,2,1,0:T(8,128)(2,1)}) custom-call(bf16[256,5120]{1,0:T(8,128)(2,1)} %bitcast.15, bf16[32,256]{1,0:T(8,128)(2,1)} %maximum_maximum_fusion.mt, bf16[5,5120,1536]{2,1,0:T(8,128)(2,1)} %wg.1, ...), custom_call_target="tpu_custom_call" | custom-call | flops 88583700480 | bytes 188743680 | tf_op jit(solution)/shard_map/pallas_call | solution.py:256
  131.5 106.4 %shard_map.101 = bf16[256,5120]{1,0:T(8,128)(2,1)} custom-call(bf16[5,512,1536]{2,1,0:T(8,128)(2,1)} %get-tuple-element.8.h, bf16[256,1536]{1,0:T(8,128)(2,1)} %get-tuple-element.9.hs, bf16[8,320,256]{2,1,0:T(8,128)(2,1)} %get-tuple-element.10.gt, bf16[5,1536,5120]{2,1,0:T(8,128)(2,1)} %wd.1, bf16[1536,5120]{1,0:T(8,128)(2,1)} %sd.1), custom_call_target="tpu_custom_call" | custom-call | flops 44291850240 | bytes 94371840 | tf_op jit(solution)/shard_map/pallas_call | solution.py:447
  237.9 3.4 %copy.12 = bf16[1,1,256,5120]{3,2,1,0:T(8,128)(2,1)} copy(bf16[1,1,256,5120]{3,2,1,0:T(8,128)(2,1)} %bitcast.14) | data formatting | bytes 5242880
  (1 shorter events, 0.0 us)

commit v4 on v3

--- a/solution.py
+++ b/solution.py
@@ -44,7 +44,7 @@
     pltpu.make_async_copy(ref, ref, sem).wait()
 
 
-def up_kernel(n, local, slots, x, mt, wg, wu, sg, su, h, hs, gt, xg, acc_g, acc_u, wbuf, xv, z, dm, gm, meta, hst,
+def up_kernel(n, local, slots, x, expert, slot_in, gate, wg, wu, sg, su, h, hs, gt, xg, acc_g, acc_u, wbuf, xv, z, dm, gm, meta, hst,
               meta_send, meta_recv, own_send, fwd_send, pass_send, recv_l, recv_r, recv_a, recv_b, recv_p,
               wsem, xsem, ldsem, osem):
     me, chips, chip, core, right, left, across = places(n)
@@ -54,7 +54,7 @@
     chunks = d // WIDTH
     half = tokens // 2
     rows = n * slots
-    top = mt.shape[0] // 4
+    top = expert.shape[0]
 
     def cols(c):
         return pl.ds(pl.multiple_of(c * WIDTH, WIDTH), WIDTH)
@@ -77,29 +77,37 @@
     for c in range(chunks):
         pltpu.make_async_copy(x.at[:, cols(c)], piece(c), xsem.at[c]).start()
 
+    mine = core * chips + chip
+    known = [expert[...].astype(F32), jnp.minimum(slot_in[...], slots).astype(F32), gate[...]]
+    known.append(jnp.zeros((top, tokens), F32))
+    meta[mine] = jnp.concatenate(known).astype(BF16)
+
     barrier = pltpu.get_barrier_semaphore()
     for r in range(1, n):
         pl.semaphore_signal(barrier, inc=1, device_id={"ep": lax.rem(me + r, n)}, device_id_type=MESH)
     pl.semaphore_wait(barrier, n - 1)
 
-    mine = core * chips + chip
-
-    def own(c, i):
-        part = pl.ds(i * half, half)
-        src, dst = x.at[part, cols(c)], xg.at[c, core, chip, part]
-        send(src, dst, own_send.at[0], recv_l.at[c], dev_r)
-        send(src, dst, own_send.at[1], recv_r.at[c], dev_l)
+    upper, lower = pl.ds(0, half), pl.ds(half, half)
+
+    def own(c):
+        src, dst = x.at[:, cols(c)], xg.at[c, core, chip]
+        for i, (to_r, to_l) in enumerate(((upper, lower), (lower, upper))):
+            send(src.at[to_r], dst.at[to_r], own_send.at[0], recv_l.at[c, i], dev_r)
+            send(src.at[to_l], dst.at[to_l], own_send.at[1], recv_r.at[c, i], dev_l)
         send(src, dst, own_send.at[2], recv_p.at[c], dev_p)
 
     def forward(c):
+        from_l, from_r = xg.at[c, core, left, upper], xg.at[c, core, right, lower]
+        wait(from_l, recv_l.at[c, 0])
+        send(from_l, from_l, fwd_send.at[0], recv_a.at[c], dev_r)
+        wait(from_r, recv_r.at[c, 0])
+        send(from_r, from_r, fwd_send.at[1], recv_b.at[c], dev_l)
+
+    def hand_over(c):
         piece_l, piece_r = xg.at[c, core, left], xg.at[c, core, right]
-        wait(piece_l, recv_l.at[c])
-        upper = piece_l.at[pl.ds(0, half)]
-        send(upper, upper, fwd_send.at[0], recv_a.at[c], dev_r)
-        wait(piece_r, recv_r.at[c])
-        lower = piece_r.at[pl.ds(half, half)]
-        send(lower, lower, fwd_send.at[1], recv_b.at[c], dev_l)
+        wait(piece_l.at[lower], recv_l.at[c, 1])
         send(piece_l, piece_l, pass_send.at[0], recv_p.at[c], dev_p)
+        wait(piece_r.at[upper], recv_r.at[c, 1])
         send(piece_r, piece_r, pass_send.at[1], recv_p.at[c], dev_p)
 
     def last_hop(c):
@@ -116,11 +124,9 @@
         for other in (left, right, across):
             pltpu.make_async_copy(xg.at[c, core, other], xv.at[slot, core, other], ldsem.at[slot]).start()
 
-    own(0, 0)
-    own(0, 1)
+    own(0)
     for r in range(1, n):
-        send(mt, meta.at[mine], meta_send.at[r], meta_recv.at[mine], lax.rem(me + r, n))
-    meta[mine] = mt[...]
+        send(meta.at[mine], meta.at[mine], meta_send.at[r], meta_recv.at[mine], lax.rem(me + r, n))
 
     tiles = [(i, min(i + TILE, ff)) for i in range(0, ff, TILE)]
 
@@ -138,43 +144,43 @@
                 v = mm(xc, wbuf[slot, k, :, lo:hi])
                 acc[0, :tokens, lo:hi] = v if c == 0 else acc[0, :tokens, lo:hi] + v
 
+    def build():
+        for r in range(1, n):
+            src = lax.rem(me + r, n)
+            q = lax.rem(src, 2) * chips + lax.div(src, 2)
+            wait(meta.at[q], meta_recv.at[q])
+        first = (me * local).astype(F32)
+
+        @pl.loop(0, n)
+        def _(q):
+            m = meta[q].astype(F32)
+            e, s, g = m[0:top], m[top : 2 * top], m[2 * top : 3 * top]
+            row = lax.broadcasted_iota(jnp.int32, (slots, tokens), 0).astype(F32)
+            for i in range(local):
+                chosen = e == first + float(i)
+                place = jnp.max(jnp.where(chosen, s, -1.0), axis=0, keepdims=True)
+                share = jnp.sum(jnp.where(chosen, g, 0.0), axis=0, keepdims=True)
+                hit = row == place
+                hot = jnp.where(hit, 1.0, 0.0)
+                weight = jnp.where(hit, share, 0.0)
+                dm[q, i * slots : (i + 1) * slots] = hot.astype(BF16)
+                gm[q, i * slots : (i + 1) * slots] = weight.astype(BF16)
+
     for c in range(chunks):
+        if c == chunks - 1:
+            build()
+        if c == chunks - 4:
+            forward(0)
+            own(1)
         if c == chunks - 2:
-            forward(0)
-            own(1, 0)
-            own(1, 1)
-            own(2, 0)
+            hand_over(0)
         shared_step(c)
+    last_hop(0)
     hst[0, :tokens] = (silu(acc_g[0, :tokens]) * acc_u[0, :tokens]).astype(BF16)
     pltpu.make_async_copy(hst.at[0, pl.ds(0, tokens)], hs, osem.at[0]).start()
-
-    for r in range(1, n):
-        src = lax.rem(me + r, n)
-        q = lax.rem(src, 2) * chips + lax.div(src, 2)
-        wait(meta.at[q], meta_recv.at[q])
-    first = (me * local).astype(F32)
-
-    @pl.loop(0, n)
-    def _(q):
-        m = meta[q].astype(F32)
-        e, s, g = m[0:top], m[top : 2 * top], m[2 * top : 3 * top]
-        ok = (e >= first) & (e < first + local) & (s < slots)
-        key = jnp.where(ok, (e - first) * slots + s, -1.0)
-        for i in range(local):
-            row = lax.broadcasted_iota(jnp.int32, (slots, tokens), 0).astype(F32) + float(i * slots)
-            hot = jnp.zeros((slots, tokens), F32)
-            weight = jnp.zeros((slots, tokens), F32)
-            for k in range(top):
-                hit = row == key[k : k + 1]
-                hot = jnp.where(hit, 1.0, hot)
-                weight = jnp.where(hit, g[k : k + 1], weight)
-            dm[q, i * slots : (i + 1) * slots] = hot.astype(BF16)
-            gm[q, i * slots : (i + 1) * slots] = weight.astype(BF16)
-
-    last_hop(0)
     pltpu.make_async_copy(gm, gt, osem.at[1]).start()
+    load(0)
     wait(hs, osem.at[0])
-    load(0)
 
     def dispatch(c):
         slot = lax.rem(c, 2)
@@ -190,17 +196,14 @@
 
         @pl.when(c + 2 < chunks)
         def _():
-            own(c + 2, 1)
-
-        @pl.when(c + 3 < chunks)
-        def _():
-            own(c + 3, 0)
+            own(c + 2)
 
         start, groups = 0, (local - 2, 1, 1)
         for i, size in enumerate(groups):
             group = range(start, start + size)
             start += size
             if i == 1:
+                hand_over(c + 1)
                 last_hop(c + 1)
             if i == 2:
                 load(c + 1)
@@ -243,10 +246,10 @@
     for i in range(2):
         wait(x.at[pl.ds(0, half)], fwd_send.at[i])
     for r in range(1, n):
-        wait(mt, meta_send.at[r])
-
-
-def up(n, slots, x, mt, wg, wu, sg, su):
+        wait(meta.at[mine], meta_send.at[r])
+
+
+def up(n, slots, x, expert, slot, gate, wg, wu, sg, su):
     tokens, d = x.shape
     local, _, ff = wg.shape
     chunks, rows, chips = d // WIDTH, n * slots, n // 2
@@ -261,7 +264,7 @@
             jax.ShapeDtypeStruct((n, local * slots, tokens), BF16),
             jax.ShapeDtypeStruct((chunks, 2, chips, tokens, WIDTH), BF16),
         ],
-        in_specs=[ANY, VM, ANY, ANY, ANY, ANY],
+        in_specs=[ANY, VM, VM, VM, ANY, ANY, ANY, ANY],
         out_specs=[ANY] * 4,
         scratch_shapes=[
             pltpu.VMEM((local, rows, ff), F32),
@@ -271,17 +274,17 @@
             pltpu.VMEM((local, rows, WIDTH), BF16),
             pltpu.VMEM((n, local * slots, tokens), BF16),
             pltpu.VMEM((n, local * slots, tokens), BF16),
-            pltpu.VMEM((n, *mt.shape), BF16),
+            pltpu.VMEM((n, 4 * expert.shape[0], tokens), BF16),
             pltpu.VMEM((2, rows, ff), BF16),
             dma((n,)), dma((n,)), dma((3,)), dma((2,)), dma((3,)),
-            dma((chunks,)), dma((chunks,)), dma((chunks,)), dma((chunks,)), dma((chunks,)),
+            dma((chunks, 2)), dma((chunks, 2)), dma((chunks,)), dma((chunks,)), dma((chunks,)),
             dma((local,)), dma((chunks,)), dma((2,)), dma((4,)),
         ],
         compiler_params=pltpu.CompilerParams(
             collective_id=0, has_side_effects=True, vmem_limit_bytes=66 * 10**6
         ),
         cost_estimate=pl.CostEstimate(flops=flops, bytes_accessed=moved, transcendentals=0),
-    )(x, mt, wg, wu, sg, su)
+    )(x, expert, slot, gate, wg, wu, sg, su)
 
 
 def down_kernel(n, local, slots, h, hs, gt, wd, sd, y, hv, hsv, gm, wbuf, outs, part, sh, pair_s, pair_r, hop_s, hop_r,
@@ -309,10 +312,10 @@
         def _():
             pltpu.make_async_copy(sd.at[:, cols(c)], wbuf.at[slot], wsem.at[slot]).start()
 
-    fetch(jnp.int32(0))
     for e in range(local):
         pltpu.make_async_copy(h.at[e], hv.at[e], insem.at[e]).start()
-    fetch(jnp.int32(1))
+        if e < 2:
+            fetch(jnp.int32(e))
     pltpu.make_async_copy(hs, hsv, insem.at[local]).start()
     pltpu.make_async_copy(gt, gm, insem.at[local + 1]).start()
 
@@ -481,9 +484,7 @@
         x, expert, slot, gate = x[0, 0], expert[0, 0], slot[0, 0], gate[0, 0]
         (tokens, top), local = expert.shape, w_gate.shape[0]
         slots = 5 * tokens * top // (4 * local * n)
-        parts = [expert.astype(BF16), jnp.minimum(slot, slots).astype(BF16), gate.astype(BF16)]
-        mt = jnp.concatenate([p.T for p in parts] + [jnp.zeros((top, tokens), BF16)])
-        h, hs, gt, _ = up(n, slots, x, mt, w_gate, w_up, s_gate, s_up)
+        h, hs, gt, _ = up(n, slots, x, expert.T, slot.T, gate.T, w_gate, w_up, s_gate, s_up)
         return down(n, slots, h, hs, gt, w_down, s_down)[None, None]
 
     a, e, r = P("dp", "ep", None, None), P("ep", None, None), P(None, None)

time: 242 us -> 235 us (0.971)
  Pallas kernels: 236 us -> 232 us
    pallas_call x1, Pallas kernels: 129 us -> 125 us  [up(): pl.pallas_call(functools.partial(up_kernel, n, local, slots), out_shape=[...]
where the time goes in v4:
time: 235 us
  Pallas kernels  232 us (99%)
  local copies, waits for them, and re-layouts  3.4 us (1%)
    pallas_call x1, Pallas kernels, up(): pl.pallas_call(functools.partial(up_kernel, n, local, slots), out_shape=[...  125 us
    pallas_call x1, Pallas kernels, down(): pl.pallas_call(functools.partial(down_kernel, n, local, slots), out_shape...  107 us

profile of v4, /device:TPU:112, one launch (start us, length us, event | category | flops | bytes accessed | tf_op | source)
XLA Modules:
  0.0 235.1 jit_solution(4869120613664978514)
XLA Ops:
  0.0 125.0 %shard_map.100 = (bf16[5,512,1536]{2,1,0:T(8,128)(2,1)}, bf16[256,1536]{1,0:T(8,128)(2,1)}, bf16[8,320,256]{2,1,0:T(8,128)(2,1)}, bf16[10,2,4,256,512]{4,3,2,1,0:T(8,128)(2,1)}) custom-call(bf16[256,5120]{1,0:T(8,128)(2,1)} %bitcast.12, s32[8,256]{1,0:T(8,128)} %bitcast.13, s32[8,256]{1,0:T(8,128)} %bitcast.14, f32[8,256]{1,0:T(8,128)} %bitcast.15, ...), custom_call_target="tpu_custom_call" | custom-call | flops 88583700480 | bytes 188743680 | tf_op jit(solution)/shard_map/pallas_call | solution.py:259
  125.0 106.7 %shard_map.101 = bf16[256,5120]{1,0:T(8,128)(2,1)} custom-call(bf16[5,512,1536]{2,1,0:T(8,128)(2,1)} %get-tuple-element.8.h, bf16[256,1536]{1,0:T(8,128)(2,1)} %get-tuple-element.9.hs, bf16[8,320,256]{2,1,0:T(8,128)(2,1)} %get-tuple-element.10.gt, bf16[5,1536,5120]{2,1,0:T(8,128)(2,1)} %wd.1, bf16[1536,5120]{1,0:T(8,128)(2,1)} %sd.1), custom_call_target="tpu_custom_call" | custom-call | flops 44291850240 | bytes 94371840 | tf_op jit(solution)/shard_map/pallas_call | solution.py:450
  231.7 3.4 %copy.12 = bf16[1,1,256,5120]{3,2,1,0:T(8,128)(2,1)} copy(bf16[1,1,256,5120]{3,2,1,0:T(8,128)(2,1)} %bitcast.11) | data formatting | bytes 5242880
